TPU v7x, 256 devices: a whole 4x4x8 slice. The times are simulated.
256 devices in a mesh: dp: 32 (over z, y), mp: 8 (over x, core).
Axes of the slice: x: 4, y: 4, z: 8, core: 2. Of those that a mesh axis runs over, the one named last changes fastest.
Arguments:
- embedded: bfloat16 [128, 64, 4096], P('dp', None, 'mp'), may hold values from -6 to 6
- targets: int32 [128, 64], P('dp'), may hold values from 0 to 65535
- labels: int32 [128], P('dp'), may hold values from 0 to 21
- counts: int32 [32], replicated, may hold values from 0 to 4, as said below
- destinations: int32 [128], P('dp'), may hold values from 0 to 63, as said below
- gain_in: float32 [4096], replicated, may hold values from 0.1 to 1.9
- w_query: bfloat16 [4096, 2048], P(None, 'mp'), may hold values from -40 to 40
- w_key: bfloat16 [4096, 1024], P(None, 'mp'), may hold values from -0.09375 to 0.09375
- w_value: bfloat16 [4096, 1024], P(None, 'mp'), may hold values from -0.09375 to 0.09375
- w_out: bfloat16 [2048, 4096], P('mp'), may hold values from -0.5 to 0.5
- gain_out: float32 [4096], replicated, may hold values from 0.1 to 1.9
- w_vocab: bfloat16 [4096, 65536], P('mp', 'dp'), may hold values from -40 to 40
- prev_probs: float32 [22], replicated, may hold values from 0.03 to 0.2
- log_weights: float32 [22], replicated, may hold values from -200 to 21000
Outputs:
- token_loss: float32 [4096], P(('dp', 'mp'))
- new_weights: float32 [22], replicated
- probs: float32 [22], replicated
Inputs may be any that keep to these rules, and one draw needn't show every extreme that they name: The counts sum to 64. `destinations`: each value from 0 to 63 is held by exactly one live slot; entries of slots that are not live are meaningless.
All inputs are finite; a program needn't handle non-finite values.
Results may differ from a plain program's by a relative error of at most 0.015.
The roundings to bfloat16 on the way count: a program that leaves them out, or rounds other values in their place, can miss the bound.
Values may be sent and summed in bfloat16 or wider, within the bound.
No kernel may reach another device: no remote copies, remote signals or barrier semaphores. Data moves between devices by JAX's collectives and lax.ppermute only.
A program may use at most 128 MiB of HBM per device.

v0:
```python
import math
import jax
import jax.numpy as jnp
from jax import lax
from jax.sharding import Mesh
from jax.sharding import PartitionSpec as P

HEAD_DIM = 128
DOMAINS = 22
SEQ_DEV = 2
DP = ("dp_0", "dp_1")
MP = ("mp_0", "mp_1")
DP_MP = ("dp_0", "dp_1", "mp_0", "mp_1")
norm_eps = 1e-05
rope_base = 500000.0
memory_rate = 0.9
step_rate = 0.02
explore_mass = 0.005


def side_by_side(arrays, axis, dim, along):
    widths = [math.prod(a.shape[along:]) for a in arrays]
    both = jnp.concatenate(
        [a.reshape(*a.shape[:along], w) for a, w in zip(arrays, widths)], axis=along
    )
    out = lax.all_gather(both, axis, axis=dim, tiled=True)
    parts = jnp.split(out, [sum(widths[:k]) for k in range(1, len(widths))], axis=along)
    return tuple((b.reshape(*out.shape[:along], *a.shape[along:]) for a, b in zip(arrays, parts)))


def sent_to_all(array, axis):
    length = lax.axis_size(axis)
    return lax.all_to_all(
        jnp.broadcast_to(array[None], (length, *array.shape)), axis, 0, 0, tiled=True
    )


def in_order(parts, dim):
    dims = list(parts.shape[1:])
    dims[dim] *= parts.shape[0]
    return jnp.moveaxis(parts, 0, dim).reshape(dims)


def gathered_copies(array, axis, dim):
    parts = sent_to_all(array, axis)
    return in_order(parts, dim)


def split_up(array, dim, length):
    dims = array.shape
    parts = array.reshape(*dims[:dim], length, dims[dim] // length, *dims[dim + 1 :])
    return jnp.moveaxis(parts, dim, 0)


def sum_at_owner(array, axis, dim):
    length = lax.axis_size(axis)
    parts = lax.all_to_all(split_up(array, dim, length), axis, 0, 0, tiled=True)
    return jnp.sum(parts.astype(jnp.float32), axis=0)


def gathered_by_axis(array, axes, dim):
    out = array
    for number in range(len(axes) - 1, -1, -1):
        out = lax.all_gather(out, axes[number], axis=dim, tiled=True)
    return out


def stacked_from(array, axes, sequence):
    parts = array[None]
    for k in sequence:
        parts = lax.all_gather(parts, axes[k], axis=0, tiled=True)
    held = [lax.axis_size(axes[k]) for k in reversed(sequence)]
    parts = parts.reshape(*held, *array.shape)
    turned = sorted(range(len(sequence)), key=lambda place: sequence[len(sequence) - 1 - place])
    return parts.transpose(*turned, *range(len(sequence), parts.ndim)).reshape(-1, *array.shape)


def gather_axes(array, axes, sequence, dim):
    return in_order(stacked_from(array, axes, sequence), dim)


def gathered_once(array, axis):
    leaves = jax.tree.leaves(array)
    sequence = sorted(range(len(leaves)), key=lambda k: -leaves[k].size)
    width = (1, *leaves[sequence[0]].shape)[-1]
    lines = [
        jnp.pad(leaves[k].reshape(-1), (0, -leaves[k].size % width)).reshape(-1, width)
        for k in sequence
    ]
    both, at, found = (sent_to_all(jnp.concatenate(lines), axis), 0, {})
    for k, line in zip(sequence, lines):
        piece = both[:, at : at + len(line)].reshape(len(both), -1)
        found[k] = piece[:, : leaves[k].size].reshape(-1, *leaves[k].shape)
        at += len(line)
    numbers = iter(range(len(leaves)))
    return jax.tree.map(lambda _: found[next(numbers)], array)


def combined_pairwise(pieces, combine):
    while len(jax.tree.leaves(pieces)[0]) > 1:
        pieces = jax.vmap(combine)(
            *(jax.tree.map(lambda part: part[side::2], pieces) for side in (0, 1))
        )
    return jax.tree.map(lambda part: part[0], pieces)


def merged_2(array, axis, combine):
    pieces = gathered_once(array, axis)
    return combined_pairwise(pieces, combine)


def over_copies(array, axis):
    everything = sent_to_all(array, axis)
    return jnp.sum(everything, axis=0)


def packed_total(arrays, axis):
    ends = [0]
    for a in arrays:
        ends.append(ends[-1] + a.size)
    so_far = over_copies(jnp.concatenate([a.ravel() for a in arrays]), axis)
    return tuple((so_far[b:e].reshape(a.shape) for a, b, e in zip(arrays, ends, ends[1:])))


def normalize(values, gain_vec):
    inv_rms = lax.rsqrt(jnp.mean(values * values, axis=-1, keepdims=True) + norm_eps)
    return values * inv_rms * gain_vec


def rotate_halves(tensor):
    full_width = tensor.shape[-1]
    half_width = full_width // 2
    frequency = jnp.power(
        jnp.float32(rope_base), -jnp.arange(half_width, dtype=jnp.float32) * 2.0 / full_width
    )
    angles = jnp.arange(tensor.shape[1], dtype=jnp.float32)[:, None] * frequency[None, :]
    cosine = jnp.cos(angles)[None, :, None, :]
    sine_part = jnp.sin(angles)[None, :, None, :]
    first_half = tensor[..., :half_width]
    second = tensor[..., half_width:]
    return jnp.concatenate(
        [first_half * cosine - second * sine_part, second * cosine + first_half * sine_part],
        axis=-1,
    )


def local(
    embedded,
    targets,
    labels,
    counts,
    destinations,
    gain_in,
    w_query,
    w_key,
    w_value,
    w_out,
    gain_out,
    w_vocab,
    prev_probs,
    log_weights,
):
    data_count = lax.axis_size(DP)
    data_index = lax.axis_index(DP)
    model_shard_count = lax.axis_size(MP)
    model_index = lax.axis_index(MP)
    slot_count = embedded.shape[0]
    seq_len = embedded.shape[1]
    seq_held = SEQ_DEV
    gathered_rows = (
        lax.all_gather(embedded, DP, axis=0, tiled=True),
        *side_by_side((targets, labels, destinations), DP, 0, 1),
    )
    slot_ids = jnp.arange(data_count * slot_count, dtype=jnp.int32)
    is_live = slot_ids % slot_count < counts[slot_ids // slot_count]
    wanted = data_index * seq_held + jnp.arange(seq_held, dtype=jnp.int32)
    picking_mask = (gathered_rows[3][None, :] == wanted[:, None]) & is_live[None, :]
    sequence_rows = jnp.einsum(
        "av,vyr->ayr",
        picking_mask.astype(jnp.bfloat16),
        gathered_rows[0],
        preferred_element_type=jnp.float32,
    ).astype(jnp.bfloat16)
    seq_targets = jnp.einsum("gs,sl->gl", picking_mask.astype(jnp.int32), gathered_rows[1])
    seq_labels = jnp.sum(jnp.where(picking_mask, gathered_rows[2][None, :], 0), axis=1).astype(
        jnp.int32
    )
    full_rows = gathered_copies(sequence_rows, MP, 2)
    rows_all = seq_held * seq_len
    flat_rows = full_rows.reshape(rows_all, -1).astype(jnp.float32)
    normed = normalize(flat_rows, gain_in).astype(jnp.bfloat16)
    local_heads = w_query.shape[1] // HEAD_DIM
    local_groups = w_key.shape[1] // HEAD_DIM
    query_heads = jnp.dot(normed, w_query, preferred_element_type=jnp.float32).reshape(
        seq_held, seq_len, local_heads, HEAD_DIM
    )
    key_heads = jnp.dot(normed, w_key, preferred_element_type=jnp.float32).reshape(
        seq_held, seq_len, local_groups, HEAD_DIM
    )
    value_heads = (
        jnp.dot(normed, w_value, preferred_element_type=jnp.float32)
        .astype(jnp.bfloat16)
        .reshape(seq_held, seq_len, local_groups, HEAD_DIM)
    )
    query_heads = rotate_halves(query_heads).astype(jnp.bfloat16)
    key_heads = rotate_halves(key_heads).astype(jnp.bfloat16)
    group_size = local_heads // local_groups
    key_heads = jnp.repeat(key_heads, group_size, axis=2)
    value_heads = jnp.repeat(value_heads, group_size, axis=2)
    scores = jnp.einsum(
        "sqhe,skhe->shqk", query_heads, key_heads, preferred_element_type=jnp.float32
    ) * HEAD_DIM ** (-0.5)
    causal = jnp.arange(seq_len)[:, None] >= jnp.arange(seq_len)[None, :]
    scores = jnp.where(causal[None, None], scores, -jnp.inf)
    weights = jax.nn.softmax(scores, axis=-1).astype(jnp.bfloat16)
    mixed_heads = jnp.einsum(
        "shqk,skhe->sqhe", weights, value_heads, preferred_element_type=jnp.float32
    )
    mixed_heads = mixed_heads.astype(jnp.bfloat16).reshape(rows_all, local_heads * HEAD_DIM)
    row_block_tiles = rows_all // model_shard_count
    update = sum_at_owner(
        jnp.dot(mixed_heads, w_out, preferred_element_type=jnp.float32).astype(jnp.bfloat16), MP, 0
    )
    my_start = model_index * row_block_tiles
    own_rows = lax.dynamic_slice_in_dim(flat_rows, my_start, row_block_tiles, 0)
    hidden = own_rows + update
    final_rows = normalize(hidden, gain_out).astype(jnp.bfloat16)
    own_targets = lax.dynamic_slice_in_dim(
        seq_targets.reshape(rows_all), my_start, row_block_tiles, 0
    )
    own_labels = lax.dynamic_slice_in_dim(
        jnp.repeat(seq_labels, seq_len), my_start, row_block_tiles, 0
    )
    everyone = (
        gathered_by_axis(final_rows, DP, 0),
        gathered_by_axis(own_targets, DP, 0),
        gathered_by_axis(own_labels, DP, 0),
    )
    all_rows = everyone[0]
    all_goals = everyone[1]
    all_kinds = everyone[2]
    vocab_local = w_vocab.shape[1]
    logits = jnp.dot(
        all_rows, gather_axes(w_vocab, MP, (0, 1), 0), preferred_element_type=jnp.float32
    )
    row_top = jnp.max(logits, axis=1)
    spread = jnp.sum(jnp.exp(logits - row_top[:, None]), axis=1)
    column_ids = all_goals - data_index * vocab_local
    picked = jnp.sum(
        jnp.where(
            jnp.arange(vocab_local, dtype=jnp.int32)[None, :] == column_ids[:, None], logits, 0.0
        ),
        axis=1,
    )

    def combine(earlier, later):
        larger = jnp.maximum(earlier[0], later[0])
        joined = earlier[1] * jnp.exp(earlier[0] - larger) + later[1] * jnp.exp(later[0] - larger)
        return (larger, joined, earlier[2] + later[2])

    merged = merged_2((row_top, spread, picked), DP, combine)
    top_all = merged[0]
    spread_all = merged[1]
    picked_all = merged[2]
    losses = top_all + jnp.log(spread_all) - picked_all
    own_loss = lax.dynamic_slice_in_dim(losses, data_index * row_block_tiles, row_block_tiles, 0)
    domains = jnp.arange(DOMAINS, dtype=jnp.int32)
    member = (all_kinds[:, None] == domains[None, :]).astype(jnp.float32)
    totals = packed_total((jnp.sum(member * losses[:, None], axis=0), jnp.sum(member, axis=0)), MP)
    loss_sums = totals[0]
    token_tally = totals[1]
    reward = loss_sums / jnp.maximum(token_tally, 1.0) / prev_probs
    new_weights = memory_rate * log_weights + (1.0 - memory_rate) * reward
    probs = (1.0 - DOMAINS * explore_mass) * jax.nn.softmax(step_rate * new_weights) + explore_mass
    return (own_loss, new_weights, probs)


def solution(mesh):
    torus = Mesh(mesh.devices.reshape(8, 4, 4, 2), ("dp_0", "dp_1", "mp_0", "mp_1"))
    in_specs = (
        P(DP, None, MP),
        P(DP, None),
        P(DP),
        P(),
        P(DP),
        P(),
        P(None, MP),
        P(None, MP),
        P(None, MP),
        P(MP, None),
        P(),
        P(MP, DP),
        P(),
        P(),
    )
    out_specs = (P(DP_MP), P(), P())
    return jax.shard_map(local, mesh=torus, in_specs=in_specs, out_specs=out_specs, check_vma=False)
```

profile of v0, /device:TPU:1, one launch (start us, length us, event | category | flops | bytes accessed | tf_op | source)
XLA Modules:
  0.0 396.9 jit_solution(11484693053749680303)
XLA Ops:
  7.2 0.7 all-gather.13.cloned.1.call-update
  8.0 0.7 all-gather.7.cloned.1.call-update
  8.7 90.3 %all-gather.13.cloned.1.call-done = bf16[2048,2048]{1,0:T(8,128)(2,1)} async-done(((bf16[512,2048]{1,0:T(8,128)(2,1)}), bf16[2048,2048]{1,0:T(8,128)(2,1)}) %all-gather.13.cloned.1.call-update) | async-done | bytes 8388624 | tf_op jit(solution)/shard_map/all_gather | solution.py:71
  99.1 0.6 copy-done.10
  99.7 0.1 copy.86
  99.8 0.1 copy.87
  100.0 39.4 %all-gather.1 = s32[32,4,66]{2,1,0:T(4,128)S(1)} all-gather(s32[1,4,66]{2,1,0:T(4,128)S(1)} %add_bitcast_fusion), channel_id=1, replica_groups=mesh['dp_0'=8,'dp_1'=4,'mp_0'=4,'mp_1'=2] {'dp_0','dp_1'}, dimensions={0}, use_global_device_ids=true | all-gather | bytes 34848 | tf_op jit(solution)/shard_map/all_gather | solution.py:26
  139.6 1.2 gather_fusion
  140.9 0.2 select_reduce_fusion.2
  141.1 59.0 %all-gather.7.cloned.1.call-done = bf16[128,64,512]{2,1,0:T(8,128)(2,1)} async-done(((bf16[4,64,512]{2,1,0:T(8,128)(2,1)}), bf16[128,64,512]{2,1,0:T(8,128)(2,1)}) %all-gather.7.cloned.1.call-update) | async-done | bytes 8388624 | tf_op jit(solution)/shard_map/all_gather | solution.py:171
  200.0 12.2 %fusion.7 = bf16[2,64,512]{2,0,1:T(2,128)(2,1)S(1)} fusion(bf16[128,64,512]{2,1,0:T(8,128)(2,1)} %all-gather.7.cloned.1.call-done, pred[2,128]{1,0:T(4,128)(4,1)S(1)} %get-tuple-element.22), kind=kOutput, calls=%fused_computation.19 | convolution fusion | flops 16842752 | bytes 8519936 | tf_op jit(solution)/shard_map/av,vyr->ayr/dot_general | solution.py:178
  212.3 1.1 broadcast_in_dim.39
  213.4 5.7 %all-to-all-start = ((bf16[8,2,64,512]{3,2,1,0:T(8,128)(2,1)}), bf16[8,2,64,512]{3,2,1,0:T(8,128)(2,1)S(1)}, u32[]{:S(2)}, u32[]{:S(2)}) async-start(bf16[8,2,64,512]{3,2,1,0:T(8,128)(2,1)} %broadcast_in_dim.39), calls=%async_computation | async-start | bytes 2097152 | tf_op jit(solution)/shard_map/all_to_all | solution.py:33
  219.0 4.3 %copy.104 = bf16[256,4096]{1,0:T(8,128)(2,1)} copy(bf16[256,4096]{0,1:T(8,128)(2,1)} %bitcast.86) | data formatting | bytes 4194304 | tf_op jit(solution)/shard_map/dot_general | solution.py:194
  223.4 0.1 fusion.32
  223.5 10.4 %all-to-all-done = bf16[8,2,64,512]{3,2,1,0:T(8,128)(2,1)S(1)} async-done(((bf16[8,2,64,512]{3,2,1,0:T(8,128)(2,1)}), bf16[8,2,64,512]{3,2,1,0:T(8,128)(2,1)S(1)}, u32[]{:S(2)}, u32[]{:S(2)}) %all-to-all-start) | async-done | bytes 1048608 | tf_op jit(solution)/shard_map/all_to_all | solution.py:33
  234.0 1.6 convert_bitcast_fusion.1
  235.6 1.5 copy.110
  237.1 0.3 fusion.3
  237.5 0.3 fusion.13
  237.8 1.6 copy.92
  239.4 1.6 reshape.334
  241.0 2.8 copy.91
  243.8 3.0 copy.111
  246.8 0.5 convolution_bitcast_fusion
  247.5 0.9 copy-done.3
  248.4 0.9 fusion.15
  249.3 0.1 subtract_convert_fusion
  249.4 0.3 fusion.53
  249.7 0.2 fusion.11
  249.9 2.4 convolution_convert_fusion.2
  252.3 0.2 fusion.12
  252.6 1.5 convolution_convert_fusion
  254.1 4.5 %all-to-all-start.1 = ((bf16[8,16,4096]{2,1,0:T(8,128)(2,1)}), bf16[8,16,4096]{2,1,0:T(8,128)(2,1)S(1)}, u32[]{:S(2)}, u32[]{:S(2)}) async-start(bf16[8,16,4096]{2,1,0:T(8,128)(2,1)} %bitcast.19), calls=%async_computation.1 | async-start | bytes 2097152 | tf_op jit(solution)/shard_map/all_to_all | solution.py:57
  258.7 14.9 %all-to-all-done.1 = bf16[8,16,4096]{2,1,0:T(8,128)(2,1)S(1)} async-done(((bf16[8,16,4096]{2,1,0:T(8,128)(2,1)}), bf16[8,16,4096]{2,1,0:T(8,128)(2,1)S(1)}, u32[]{:S(2)}, u32[]{:S(2)}) %all-to-all-start.1) | async-done | bytes 1048608 | tf_op jit(solution)/shard_map/all_to_all | solution.py:57
  273.6 0.1 convert_reduce_fusion
  273.8 1.1 multiply_reduce_fusion
  274.9 1.0 multiply_convert_fusion.4
  276.0 10.6 %all_gather.32 = bf16[64,4096]{1,0:T(8,128)(2,1)} all-gather(bf16[16,4096]{1,0:T(8,128)(2,1)S(1)} %multiply_convert_fusion.4), channel_id=1, replica_groups=mesh['dp_0'=8,'dp_1'=4,'mp_0'=4,'mp_1'=2] {'dp_1'}, dimensions={0}, use_global_device_ids=true | all-gather | bytes 655360 | tf_op jit(solution)/shard_map/all_gather | solution.py:64
  286.6 0.2 fusion.23
  287.0 0.6 dynamic-slice.1
  287.6 0.6 dynamic-slice.2
  289.5 0.2 dynamic-slice_dynamic-update-slice_fusion.1
  289.7 0.2 dynamic-slice_dynamic-update-slice_fusion
  289.8 5.6 %all-reduce.5 = (s32[64]{0:T(128)S(1)}, s32[64]{0:T(128)S(1)}) all-reduce(s32[64]{0:T(128)S(1)} %dynamic-slice_dynamic-update-slice_fusion.1, s32[64]{0:T(128)S(1)} %dynamic-slice_dynamic-update-slice_fusion), channel_id=1, replica_groups=mesh['dp_0'=8,'dp_1'=4,'mp_0'=4,'mp_1'=2] {'dp_1'}, use_global_device_ids=true, to_apply=%add | all-reduce | flops 128 | bytes 1024
  295.4 0.2 dynamic-update-slice.1
  295.6 0.2 dynamic-update-slice.3
  295.8 9.7 %all-reduce.4 = (s32[512]{0:T(512)S(1)}, s32[512]{0:T(512)S(1)}) all-reduce(s32[512]{0:T(512)S(1)} %dynamic-update-slice.1, s32[512]{0:T(512)S(1)} %dynamic-update-slice.3), channel_id=1, replica_groups=mesh['dp_0'=8,'dp_1'=4,'mp_0'=4,'mp_1'=2] {'dp_0'}, use_global_device_ids=true, to_apply=%add.1 | all-reduce | flops 1024 | bytes 8192
  305.6 14.2 %copy.97 = bf16[4,2,512,2048]{3,2,1,0:T(8,128)(2,1)} copy(bf16[4,2,512,2048]{3,2,0,1:T(8,128)(2,1)} %bitcast.77) | data formatting | bytes 33554432 | tf_op jit(solution)/shard_map/transpose | solution.py:75
  319.7 20.8 %all-gather.9.cloned.1.call-done = bf16[512,4096]{1,0:T(8,128)(2,1)} async-done(((bf16[64,4096]{1,0:T(8,128)(2,1)}), bf16[512,4096]{1,0:T(8,128)(2,1)}) %all-gather.9.cloned.1.call-update) | async-done | bytes 4194320 | tf_op jit(solution)/shard_map/all_gather | solution.py:64
  340.6 13.1 %fusion.58 = (f32[512]{0:T(512)S(1)}, f32[512,2048]{1,0:T(8,128)S(1)}) fusion(bf16[512,4096]{1,0:T(8,128)(2,1)} %all-gather.9.cloned.1.call-done, bf16[4096,2048]{1,0:T(8,128)(2,1)} %bitcast.78), kind=kOutput, calls=%fused_computation.113 | convolution fusion | flops 8590983168 | bytes 25167872 | tf_op jit(solution)/shard_map/dot_general | solution.py:243
  353.7 1.1 exponential_reduce_fusion
  354.9 0.7 broadcast_in_dim.44
  355.6 7.0 %all-to-all-start.2 = ((f32[32,3,512]{2,1,0:T(4,128)}), f32[32,3,512]{2,1,0:T(4,128)S(1)}, u32[]{:S(2)}, u32[]{:S(2)}) async-start(f32[32,3,512]{2,1,0:T(4,128)} %broadcast_in_dim.44), calls=%async_computation.2 | async-start | bytes 524288 | tf_op jit(solution)/shard_map/all_to_all | solution.py:33
  362.6 11.2 %all-to-all-done.2 = f32[32,3,512]{2,1,0:T(4,128)S(1)} async-done(((f32[32,3,512]{2,1,0:T(4,128)}), f32[32,3,512]{2,1,0:T(4,128)S(1)}, u32[]{:S(2)}, u32[]{:S(2)}) %all-to-all-start.2) | async-done | bytes 196640 | tf_op jit(solution)/shard_map/all_to_all | solution.py:33
  373.8 0.1 fusion.51
  374.7 0.1 select_reduce_fusion.1
  374.9 0.6 broadcast_in_dim.50
  375.5 6.6 %all-to-all-start.3 = ((f32[8,1,44]{2,1,0:T(1,128)}), f32[8,1,44]{2,1,0:T(1,128)S(1)}, u32[]{:S(2)}, u32[]{:S(2)}) async-start(f32[8,1,44]{2,1,0:T(1,128)} %broadcast_in_dim.50), calls=%async_computation.3 | async-start | bytes 8192 | tf_op jit(solution)/shard_map/all_to_all | solution.py:33
  382.1 0.6 dynamic-slice_bitcast_fusion
  382.6 4.0 %all-to-all-done.3 = f32[8,1,44]{2,1,0:T(1,128)S(1)} async-done(((f32[8,1,44]{2,1,0:T(1,128)}), f32[8,1,44]{2,1,0:T(1,128)S(1)}, u32[]{:S(2)}, u32[]{:S(2)}) %all-to-all-start.3) | async-done | bytes 1440 | tf_op jit(solution)/shard_map/all_to_all | solution.py:33
  386.7 0.7 multiply_reduce_fusion.1
  387.4 1.2 fusion.50
  388.6 1.7 multiply_add_fusion.4
  (101 shorter events, 2.0 us)
Async XLA Ops:
  7.2 245.4 %copy-start = (bf16[256,4096]{1,0:T(8,128)(2,1)S(1)}, bf16[256,4096]{1,0:T(8,128)(2,1)}, u32[]{:S(2)}) copy-start(bf16[256,4096]{1,0:T(8,128)(2,1)} %param.23) | copy-start | bytes 6291460
  7.2 91.9 %all-gather.13.cloned.1.call-start = ((), (), s32[]{:S(2)}) async-start(), calls=%async_computation.7 | async-start | bytes 10485760 | tf_op jit(solution)/shard_map/all_gather | solution.py:71
  7.9 192.1 %all-gather.7.cloned.1.call-start = ((), (), s32[]{:S(2)}) async-start(), calls=%async_computation.4 | async-start | bytes 8650752 | tf_op jit(solution)/shard_map/all_gather | solution.py:171
  8.7 296.9 %all-gather.11.cloned.1.call-start = ((), (), s32[]{:S(2)}) async-start(), calls=%async_computation.6 | async-start | bytes 25165824 | tf_op jit(solution)/shard_map/all_gather | solution.py:71
  99.1 0.7 copy-start.10
  99.1 0.7 copy-start.11
  99.1 0.8 copy-start.8
  99.1 40.6 %copy-start.2 = (s32[32]{0:T(128)S(1)}, s32[32]{0:T(128)}, u32[]{:S(2)}) copy-start(s32[32]{0:T(128)} %param.17) | copy-start | bytes 388
  212.3 6.8 %copy-start.6 = (f32[4096]{0:T(1024)S(1)}, f32[4096]{0:T(1024)}, u32[]{:S(2)}) copy-start(f32[4096]{0:T(1024)} %param.19) | copy-start | bytes 49156
  213.4 20.6 %all-to-all-start = ((bf16[8,2,64,512]{3,2,1,0:T(8,128)(2,1)}), bf16[8,2,64,512]{3,2,1,0:T(8,128)(2,1)S(1)}, u32[]{:S(2)}, u32[]{:S(2)}) async-start(bf16[8,2,64,512]{3,2,1,0:T(8,128)(2,1)} %broadcast_in_dim.39), calls=%async_computation | async-start | bytes 2097152 | tf_op jit(solution)/shard_map/all_to_all | solution.py:33
  243.8 3.0 copy-start.4
  243.8 3.0 copy-start.5
  246.8 1.6 copy-start.3
  254.1 20.8 %copy-start.7 = (f32[4096]{0:T(1024)S(1)}, f32[4096]{0:T(1024)}, u32[]{:S(2)}) copy-start(f32[4096]{0:T(1024)} %param.24) | copy-start | bytes 49156
  254.1 19.5 %all-to-all-start.1 = ((bf16[8,16,4096]{2,1,0:T(8,128)(2,1)}), bf16[8,16,4096]{2,1,0:T(8,128)(2,1)S(1)}, u32[]{:S(2)}, u32[]{:S(2)}) async-start(bf16[8,16,4096]{2,1,0:T(8,128)(2,1)} %bitcast.19), calls=%async_computation.1 | async-start | bytes 2097152 | tf_op jit(solution)/shard_map/all_to_all | solution.py:57
  258.6 28.4 %copy-start.15 = (u32[256]{0:T(256)S(1)}, u32[256]{0:T(256)}, u32[]{:S(2)}) copy-start(u32[256]{0:T(256)} %constant.102) | copy-start | bytes 3076
  258.6 29.0 %copy-start.14 = (u32[256]{0:T(256)S(1)}, u32[256]{0:T(256)}, u32[]{:S(2)}) copy-start(u32[256]{0:T(256)} %constant.107) | copy-start | bytes 3076
  258.7 81.9 %all-gather.9.cloned.1.call-start = ((), (), s32[]{:S(2)}) async-start(), calls=%async_computation.5 | async-start | bytes 4718592 | tf_op jit(solution)/shard_map/all_gather | solution.py:64
  353.7 36.6 %copy-start.1 = (bf16[256,4096]{1,0:T(8,128)(2,1)S(1)}, bf16[256,4096]{1,0:T(8,128)(2,1)}, u32[]{:S(2)}) copy-start(bf16[256,4096]{1,0:T(8,128)(2,1)} %param.23) | copy-start | bytes 6291460
  354.9 31.8 %copy-start.12 = (f32[22]{0:T(128)S(1)}, f32[22]{0:T(128)}, u32[]{:S(2)}) copy-start(f32[22]{0:T(128)} %param.26) | copy-start | bytes 268
  354.9 31.8 %copy-start.13 = (f32[22]{0:T(128)S(1)}, f32[22]{0:T(128)}, u32[]{:S(2)}) copy-start(f32[22]{0:T(128)} %param.27) | copy-start | bytes 268
  355.6 18.2 %all-to-all-start.2 = ((f32[32,3,512]{2,1,0:T(4,128)}), f32[32,3,512]{2,1,0:T(4,128)S(1)}, u32[]{:S(2)}, u32[]{:S(2)}) async-start(f32[32,3,512]{2,1,0:T(4,128)} %broadcast_in_dim.44), calls=%async_computation.2 | async-start | bytes 524288 | tf_op jit(solution)/shard_map/all_to_all | solution.py:33
  375.5 11.2 %all-to-all-start.3 = ((f32[8,1,44]{2,1,0:T(1,128)}), f32[8,1,44]{2,1,0:T(1,128)S(1)}, u32[]{:S(2)}, u32[]{:S(2)}) async-start(f32[8,1,44]{2,1,0:T(1,128)} %broadcast_in_dim.50), calls=%async_computation.3 | async-start | bytes 8192 | tf_op jit(solution)/shard_map/all_to_all | solution.py:33
  387.4 3.0 copy-start.9
Sparse Core Ops, SparseCore 0:
  9.8 89.2 all-gather.12
  101.6 98.3 all-gather.6
  201.8 33.9 all-gather.10
  286.7 53.7 all-gather.8
where the time goes:
time: 398 us; the launch traced here: 397 us
  waiting for transfers between devices  212 us (53%)
  blocking collectives  65.3 us (16%)
  local copies, waits for them, and re-layouts  38.1 us (10%)
  matrix products  31.5 us (8%)
  starting transfers between devices  23.9 us (6%)
  between operations  15.4 us (4%)
  other arithmetic  10.5 us (3%)
    all_gather x2, waiting for transfers between devices, stacked_from(): parts = lax.all_gather(parts, axes[k], axis=0, tiled=True)  90.3 us
    all_gather x1, waiting for transfers between devices, local(): lax.all_gather(embedded, DP, axis=0, tiled=True)  59 us
    all_gather x1, blocking collectives, side_by_side(): out = lax.all_gather(both, axis, axis=dim, tiled=True)  39.4 us
    all_to_all x3, waiting for transfers between devices, sent_to_all(): lax.all_to_all(jnp.broadcast_to(array[None], (length, *array.shape)), axi...  25.7 us
    all_gather x1, waiting for transfers between devices, gathered_by_axis(): out = lax.all_gather(out, axes[number], axis=dim, tiled=True)  20.8 us
    all_to_all x3, starting transfers between devices, sent_to_all(): lax.all_to_all(jnp.broadcast_to(array[None], (length, *array.shape)), axi...  19.2 us
    unnamed x2, blocking collectives  15.3 us
    all_to_all x1, waiting for transfers between devices, sum_at_owner(): parts = lax.all_to_all(split_up(array, dim, length), axis, 0, 0, tiled=True)  14.9 us
  transfers between devices with their start and end apart: 8, of which 7 were waited for; matrix products, arithmetic and copies ran while one was open for 15% of the time, Pallas kernels for 0%

commit v1 on v0

--- a/solution.py
+++ b/solution.py
@@ -168,7 +168,9 @@
     seq_len = embedded.shape[1]
     seq_held = SEQ_DEV
     gathered_rows = (
-        lax.all_gather(embedded, DP, axis=0, tiled=True),
+        jnp.concatenate(
+            lax.all_to_all(jnp.stack([embedded] * lax.axis_size(DP)), DP, 0, 0), axis=0
+        ),
         *side_by_side((targets, labels, destinations), DP, 0, 1),
     )
     slot_ids = jnp.arange(data_count * slot_count, dtype=jnp.int32)

time: 398 us -> 475 us (1.19)
  blocking collectives: 65.3 us -> 178 us
  waiting for transfers between devices: 212 us -> 134 us
  local copies, waits for them, and re-layouts: 38.1 us -> 64.6 us
  starting transfers between devices: 23.9 us -> 47.2 us
  matrix products: 31.5 us -> 25.1 us
    all_gather x1, blocking collectives: 39.4 us -> 153 us  [side_by_side(): out = lax.all_gather(both, axis, axis=dim, tiled=True)]
    all_gather x1 -> x0, waiting for transfers between devices: 59 us -> none  [local(): lax.all_gather(embedded, DP, axis=0, tiled=True)]
    all_gather x2, waiting for transfers between devices: 90.3 us -> 71.4 us  [stacked_from(): parts = lax.all_gather(parts, axes[k], axis=0, tiled=True)]
    reshape x0 -> x1, local copies, waits for them, and re-layouts: none -> 12.5 us  [local(): jnp.concatenate(lax.all_to_all(jnp.stack([embedded] * lax.axis_size(DP)),...]
    all_to_all x0 -> x1, starting transfers between devices: none -> 12.2 us  [local(): lax.all_to_all(jnp.stack([embedded] * lax.axis_size(DP)), DP, 0, 0)]
    all_to_all x3, starting transfers between devices: 19.2 us -> 30.4 us  [sent_to_all(): lax.all_to_all(jnp.broadcast_to(array[None], (length, *array.shape)), axi...]
    all_to_all x0 -> x1, local copies, waits for them, and re-layouts: none -> 8.11 us  [local(): lax.all_to_all(jnp.stack([embedded] * lax.axis_size(DP)), DP, 0, 0)]
    dot_general x1, matrix products: 12.2 us -> 4.57 us  [local(): jnp.einsum('av,vyr->ayr', picking_mask.astype(jnp.bfloat16), gathered_row...]
  transfers between devices with their start and end apart: 8 -> 8, of which waited for: 7 -> 6; matrix products, arithmetic and copies ran while one was open for 15% -> 16% of each run, Pallas kernels for 0% -> 0%
where the time goes in v1:
time: 475 us; the launch traced here: 474 us
  blocking collectives  178 us (37%)
  waiting for transfers between devices  134 us (28%)
  local copies, waits for them, and re-layouts  64.6 us (14%)
  starting transfers between devices  47.2 us (10%)
  matrix products  25.1 us (5%)
  between operations  15.5 us (3%)
  other arithmetic  9.34 us (2%)
    all_gather x1, blocking collectives, side_by_side(): out = lax.all_gather(both, axis, axis=dim, tiled=True)  153 us
    all_gather x2, waiting for transfers between devices, stacked_from(): parts = lax.all_gather(parts, axes[k], axis=0, tiled=True)  71.4 us
    all_to_all x3, starting transfers between devices, sent_to_all(): lax.all_to_all(jnp.broadcast_to(array[None], (length, *array.shape)), axi...  30.4 us
    all_to_all x3, waiting for transfers between devices, sent_to_all(): lax.all_to_all(jnp.broadcast_to(array[None], (length, *array.shape)), axi...  25.9 us
    all_gather x1, waiting for transfers between devices, gathered_by_axis(): out = lax.all_gather(out, axes[number], axis=dim, tiled=True)  21.3 us
    all_to_all x1, waiting for transfers between devices, sum_at_owner(): parts = lax.all_to_all(split_up(array, dim, length), axis, 0, 0, tiled=True)  14.9 us
    transpose x1, local copies, waits for them, and re-layouts, stacked_from(): parts.transpose(*turned, *range(len(sequence), parts.ndim))  14.2 us
    unnamed x2, blocking collectives  14.2 us
  transfers between devices with their start and end apart: 8, of which 6 were waited for; matrix products, arithmetic and copies ran while one was open for 16% of the time, Pallas kernels for 0%

profile of v1, /device:TPU:1, one launch (start us, length us, event | category | flops | bytes accessed | tf_op | source)
XLA Modules:
  0.0 473.9 jit_solution(17950624504261966114)
XLA Ops:
  7.2 0.7 all-gather.10.cloned.1.call-update
  7.9 0.4 copy-done.7
  8.3 0.2 copy.92
  8.5 7.0 %stack.2 = bf16[32,4,64,512]{3,1,2,0:T(4,128)(2,1)} broadcast(bf16[4,64,512]{2,0,1:T(4,128)(2,1)S(1)} %copy.92), dimensions={1,2,3} | broadcast | bytes 8650752 | tf_op jit(solution)/shard_map/stack | solution.py:172
  15.5 12.2 %all-to-all-start = ((bf16[32,4,64,512]{3,1,2,0:T(4,128)(2,1)}), bf16[32,4,64,512]{3,1,2,0:T(4,128)(2,1)}, u32[]{:S(2)}, u32[]{:S(2)}) async-start(bf16[32,4,64,512]{3,1,2,0:T(4,128)(2,1)} %stack.2), calls=%async_computation | async-start | bytes 16777216 | tf_op jit(solution)/shard_map/all_to_all | solution.py:172
  27.7 71.4 %all-gather.10.cloned.1.call-done = bf16[2048,2048]{1,0:T(8,128)(2,1)} async-done(((bf16[512,2048]{1,0:T(8,128)(2,1)}), bf16[2048,2048]{1,0:T(8,128)(2,1)}) %all-gather.10.cloned.1.call-update) | async-done | bytes 8388624 | tf_op jit(solution)/shard_map/all_gather | solution.py:71
  99.1 0.6 copy-done.12
  100.0 153.2 %all-gather.1 = s32[32,4,66]{2,1,0:T(4,128)S(1)} all-gather(s32[1,4,66]{2,1,0:T(4,128)S(1)} %add_bitcast_fusion), channel_id=1, replica_groups=mesh['dp_0'=8,'dp_1'=4,'mp_0'=4,'mp_1'=2] {'dp_0','dp_1'}, dimensions={0}, use_global_device_ids=true | all-gather | bytes 34848 | tf_op jit(solution)/shard_map/all_gather | solution.py:26
  253.5 1.2 gather_fusion
  254.8 0.2 select_reduce_fusion.2
  254.9 8.1 %copy.93 = bf16[32,4,64,512]{3,1,0,2:T(4,128)(2,1)} copy(bf16[32,4,64,512]{3,1,2,0:T(4,128)(2,1)} %all-to-all-done) | data formatting | bytes 16777216 | tf_op jit(solution)/shard_map/all_to_all | solution.py:172
  263.1 12.5 %reshape.291 = bf16[128,64,512]{2,0,1:T(8,128)(2,1)} reshape(bf16[32,4,64,512]{3,1,0,2:T(4,128)(2,1)} %copy.93) | data formatting | bytes 16777216 | tf_op jit(solution)/shard_map/reshape | solution.py:171
  275.6 4.6 convolution_convert_fusion.1
  280.2 1.1 broadcast_in_dim.39
  281.3 16.8 %all-to-all-start.1 = ((bf16[8,2,64,512]{3,2,1,0:T(8,128)(2,1)}), bf16[8,2,64,512]{3,2,1,0:T(8,128)(2,1)S(1)}, u32[]{:S(2)}, u32[]{:S(2)}) async-start(bf16[8,2,64,512]{3,2,1,0:T(8,128)(2,1)} %broadcast_in_dim.39), calls=%async_computation.1 | async-start | bytes 2097152 | tf_op jit(solution)/shard_map/all_to_all | solution.py:33
  298.1 4.1 copy.108
  302.3 0.1 fusion.27
  302.4 10.7 %all-to-all-done.1 = bf16[8,2,64,512]{3,2,1,0:T(8,128)(2,1)S(1)} async-done(((bf16[8,2,64,512]{3,2,1,0:T(8,128)(2,1)}), bf16[8,2,64,512]{3,2,1,0:T(8,128)(2,1)S(1)}, u32[]{:S(2)}, u32[]{:S(2)}) %all-to-all-start.1) | async-done | bytes 1048608 | tf_op jit(solution)/shard_map/all_to_all | solution.py:33
  313.1 0.3 fusion.1
  313.5 0.3 fusion.8
  313.8 1.6 copy.96
  315.4 2.4 reshape.340
  317.8 0.6 convert_bitcast_fusion.1
  318.4 1.2 copy.95
  319.6 3.0 copy.115
  322.6 0.2 copy.114
  322.8 1.0 copy-done.5
  323.8 0.5 convolution_bitcast_fusion
  324.6 0.3 copy-done.4
  324.8 0.8 fusion.10
  325.8 0.3 fusion.48
  326.1 0.9 fusion.6
  327.0 2.1 convolution_convert_fusion.3
  329.0 1.2 fusion.7
  330.4 1.4 convolution_convert_fusion
  331.8 4.5 all-to-all-start.2
  336.4 14.9 %all-to-all-done.2 = bf16[8,16,4096]{2,1,0:T(8,128)(2,1)S(1)} async-done(((bf16[8,16,4096]{2,1,0:T(8,128)(2,1)}), bf16[8,16,4096]{2,1,0:T(8,128)(2,1)S(1)}, u32[]{:S(2)}, u32[]{:S(2)}) %all-to-all-start.2) | async-done | bytes 1048608 | tf_op jit(solution)/shard_map/all_to_all | solution.py:57
  351.3 0.1 convert_reduce_fusion
  351.5 1.1 multiply_reduce_fusion
  352.6 1.0 multiply_convert_fusion.4
  353.6 10.6 %all_gather.28 = bf16[64,4096]{1,0:T(8,128)(2,1)} all-gather(bf16[16,4096]{1,0:T(8,128)(2,1)S(1)} %multiply_convert_fusion.4), channel_id=1, replica_groups=mesh['dp_0'=8,'dp_1'=4,'mp_0'=4,'mp_1'=2] {'dp_1'}, dimensions={0}, use_global_device_ids=true | all-gather | bytes 655360 | tf_op jit(solution)/shard_map/all_gather | solution.py:64
  364.3 0.6 dynamic-slice.2
  364.9 0.6 dynamic-slice.1
  365.5 0.2 fusion.18
  367.2 0.2 dynamic-slice_dynamic-update-slice_fusion.1
  367.4 0.2 dynamic-slice_dynamic-update-slice_fusion
  367.5 5.3 %all-reduce.5 = (s32[64]{0:T(128)S(1)}, s32[64]{0:T(128)S(1)}) all-reduce(s32[64]{0:T(128)S(1)} %dynamic-slice_dynamic-update-slice_fusion.1, s32[64]{0:T(128)S(1)} %dynamic-slice_dynamic-update-slice_fusion), channel_id=1, replica_groups=mesh['dp_0'=8,'dp_1'=4,'mp_0'=4,'mp_1'=2] {'dp_1'}, use_global_device_ids=true, to_apply=%add | all-reduce | flops 128 | bytes 1024
  372.8 0.2 dynamic-update-slice.1
  373.0 0.2 dynamic-update-slice.3
  373.2 8.9 %all-reduce.4 = (s32[512]{0:T(512)S(1)}, s32[512]{0:T(512)S(1)}) all-reduce(s32[512]{0:T(512)S(1)} %dynamic-update-slice.1, s32[512]{0:T(512)S(1)} %dynamic-update-slice.3), channel_id=1, replica_groups=mesh['dp_0'=8,'dp_1'=4,'mp_0'=4,'mp_1'=2] {'dp_0'}, use_global_device_ids=true, to_apply=%add.1 | all-reduce | flops 1024 | bytes 8192
  382.1 14.2 %copy.101 = bf16[4,2,512,2048]{3,2,1,0:T(8,128)(2,1)} copy(bf16[4,2,512,2048]{3,2,0,1:T(8,128)(2,1)} %bitcast.80) | data formatting | bytes 33554432 | tf_op jit(solution)/shard_map/transpose | solution.py:75
  396.3 21.3 %all-gather.6.cloned.1.call-done = bf16[512,4096]{1,0:T(8,128)(2,1)} async-done(((bf16[64,4096]{1,0:T(8,128)(2,1)}), bf16[512,4096]{1,0:T(8,128)(2,1)}) %all-gather.6.cloned.1.call-update) | async-done | bytes 4194320 | tf_op jit(solution)/shard_map/all_gather | solution.py:64
  417.6 13.1 %fusion.53 = (f32[512]{0:T(512)S(1)}, f32[512,2048]{1,0:T(8,128)S(1)}) fusion(bf16[512,4096]{1,0:T(8,128)(2,1)} %all-gather.6.cloned.1.call-done, bf16[4096,2048]{1,0:T(8,128)(2,1)} %bitcast.81), kind=kOutput, calls=%fused_computation.111 | convolution fusion | flops 8590983168 | bytes 25167872 | tf_op jit(solution)/shard_map/dot_general | solution.py:245
  430.8 1.1 exponential_reduce_fusion
  431.9 0.7 broadcast_in_dim.44
  432.7 7.0 %all-to-all-start.3 = ((f32[32,3,512]{2,1,0:T(4,128)}), f32[32,3,512]{2,1,0:T(4,128)S(1)}, u32[]{:S(2)}, u32[]{:S(2)}) async-start(f32[32,3,512]{2,1,0:T(4,128)} %broadcast_in_dim.44), calls=%async_computation.3 | async-start | bytes 524288 | tf_op jit(solution)/shard_map/all_to_all | solution.py:33
  439.6 11.2 %all-to-all-done.3 = f32[32,3,512]{2,1,0:T(4,128)S(1)} async-done(((f32[32,3,512]{2,1,0:T(4,128)}), f32[32,3,512]{2,1,0:T(4,128)S(1)}, u32[]{:S(2)}, u32[]{:S(2)}) %all-to-all-start.3) | async-done | bytes 196640 | tf_op jit(solution)/shard_map/all_to_all | solution.py:33
  451.9 0.6 broadcast_in_dim.50
  452.5 6.6 %all-to-all-start.4 = ((f32[8,1,44]{2,1,0:T(1,128)}), f32[8,1,44]{2,1,0:T(1,128)S(1)}, u32[]{:S(2)}, u32[]{:S(2)}) async-start(f32[8,1,44]{2,1,0:T(1,128)} %broadcast_in_dim.50), calls=%async_computation.4 | async-start | bytes 8192 | tf_op jit(solution)/shard_map/all_to_all | solution.py:33
  459.1 0.6 dynamic-slice_bitcast_fusion
  459.7 4.0 all-to-all-done.4
  463.8 0.7 multiply_reduce_fusion.1
  464.4 1.2 fusion.45
  465.7 1.7 multiply_add_fusion.4
  (108 shorter events, 2.6 us)
Async XLA Ops:
  7.2 323.2 %copy-start = (bf16[256,4096]{1,0:T(8,128)(2,1)S(1)}, bf16[256,4096]{1,0:T(8,128)(2,1)}, u32[]{:S(2)}) copy-start(bf16[256,4096]{1,0:T(8,128)(2,1)} %param.23) | copy-start | bytes 6291460
  7.2 1.1 copy-start.7
  7.2 91.9 %all-gather.10.cloned.1.call-start = ((), (), s32[]{:S(2)}) async-start(), calls=%async_computation.7 | async-start | bytes 10485760 | tf_op jit(solution)/shard_map/all_gather | solution.py:71
  15.5 239.5 %all-to-all-start = ((bf16[32,4,64,512]{3,1,2,0:T(4,128)(2,1)}), bf16[32,4,64,512]{3,1,2,0:T(4,128)(2,1)}, u32[]{:S(2)}, u32[]{:S(2)}) async-start(bf16[32,4,64,512]{3,1,2,0:T(4,128)(2,1)} %stack.2), calls=%async_computation | async-start | bytes 16777216 | tf_op jit(solution)/shard_map/all_to_all | solution.py:172
  27.6 354.5 %all-gather.8.cloned.1.call-start = ((), (), s32[]{:S(2)}) async-start(), calls=%async_computation.6 | async-start | bytes 25165824 | tf_op jit(solution)/shard_map/all_gather | solution.py:71
  99.1 0.7 copy-start.12
  99.1 0.7 copy-start.13
  99.1 0.8 copy-start.10
  99.1 154.4 %copy-start.2 = (s32[32]{0:T(128)S(1)}, s32[32]{0:T(128)}, u32[]{:S(2)}) copy-start(s32[32]{0:T(128)} %param.17) | copy-start | bytes 388
  280.1 18.0 %copy-start.8 = (f32[4096]{0:T(1024)S(1)}, f32[4096]{0:T(1024)}, u32[]{:S(2)}) copy-start(f32[4096]{0:T(1024)} %param.19) | copy-start | bytes 49156
  281.3 31.8 %all-to-all-start.1 = ((bf16[8,2,64,512]{3,2,1,0:T(8,128)(2,1)}), bf16[8,2,64,512]{3,2,1,0:T(8,128)(2,1)S(1)}, u32[]{:S(2)}, u32[]{:S(2)}) async-start(bf16[8,2,64,512]{3,2,1,0:T(8,128)(2,1)} %broadcast_in_dim.39), calls=%async_computation.1 | async-start | bytes 2097152 | tf_op jit(solution)/shard_map/all_to_all | solution.py:33
  322.6 1.2 copy-start.5
  322.8 1.7 copy-start.3
  322.8 2.0 copy-start.4
  324.8 2.1 copy-start.6
  331.8 20.8 %copy-start.9 = (f32[4096]{0:T(1024)S(1)}, f32[4096]{0:T(1024)}, u32[]{:S(2)}) copy-start(f32[4096]{0:T(1024)} %param.24) | copy-start | bytes 49156
  331.8 19.5 %all-to-all-start.2 = ((bf16[8,16,4096]{2,1,0:T(8,128)(2,1)}), bf16[8,16,4096]{2,1,0:T(8,128)(2,1)S(1)}, u32[]{:S(2)}, u32[]{:S(2)}) async-start(bf16[8,16,4096]{2,1,0:T(8,128)(2,1)} %bitcast.19), calls=%async_computation.2 | async-start | bytes 2097152 | tf_op jit(solution)/shard_map/all_to_all | solution.py:57
  336.3 28.0 %copy-start.17 = (u32[256]{0:T(256)S(1)}, u32[256]{0:T(256)}, u32[]{:S(2)}) copy-start(u32[256]{0:T(256)} %constant.107) | copy-start | bytes 3076
  336.3 28.6 %copy-start.16 = (u32[256]{0:T(256)S(1)}, u32[256]{0:T(256)}, u32[]{:S(2)}) copy-start(u32[256]{0:T(256)} %constant.102) | copy-start | bytes 3076
  336.3 81.3 %all-gather.6.cloned.1.call-start = ((), (), s32[]{:S(2)}) async-start(), calls=%async_computation.5 | async-start | bytes 4718592 | tf_op jit(solution)/shard_map/all_gather | solution.py:64
  430.8 36.6 %copy-start.1 = (bf16[256,4096]{1,0:T(8,128)(2,1)S(1)}, bf16[256,4096]{1,0:T(8,128)(2,1)}, u32[]{:S(2)}) copy-start(bf16[256,4096]{1,0:T(8,128)(2,1)} %param.23) | copy-start | bytes 6291460
  431.9 31.9 %copy-start.14 = (f32[22]{0:T(128)S(1)}, f32[22]{0:T(128)}, u32[]{:S(2)}) copy-start(f32[22]{0:T(128)} %param.26) | copy-start | bytes 268
  431.9 31.9 %copy-start.15 = (f32[22]{0:T(128)S(1)}, f32[22]{0:T(128)}, u32[]{:S(2)}) copy-start(f32[22]{0:T(128)} %param.27) | copy-start | bytes 268
  432.7 18.2 %all-to-all-start.3 = ((f32[32,3,512]{2,1,0:T(4,128)}), f32[32,3,512]{2,1,0:T(4,128)S(1)}, u32[]{:S(2)}, u32[]{:S(2)}) async-start(f32[32,3,512]{2,1,0:T(4,128)} %broadcast_in_dim.44), calls=%async_computation.3 | async-start | bytes 524288 | tf_op jit(solution)/shard_map/all_to_all | solution.py:33
  452.5 11.2 %all-to-all-start.4 = ((f32[8,1,44]{2,1,0:T(1,128)}), f32[8,1,44]{2,1,0:T(1,128)S(1)}, u32[]{:S(2)}, u32[]{:S(2)}) async-start(f32[8,1,44]{2,1,0:T(1,128)} %broadcast_in_dim.50), calls=%async_computation.4 | async-start | bytes 8192 | tf_op jit(solution)/shard_map/all_to_all | solution.py:33
  464.4 2.9 copy-start.11
Sparse Core Ops, SparseCore 0:
  9.8 89.2 all-gather.9
  100.9 37.2 all-gather.7
  364.4 53.1 all-gather.5
